TPU v7x, 32 devices: a whole 2x2x4 slice. The times are simulated.
32 devices in a mesh: dp: 4 (over x, core), mp: 8 (over z, y).
Axes of the slice: x: 2, y: 2, z: 4, core: 2. Of those that a mesh axis runs over, the one named last changes fastest.
Arguments:
- tokens: bfloat16 [1280, 1792], P(('dp', 'mp')), may hold values from -6 to 6
- norm_gain: float32 [1792], replicated, may hold values from 0.5 to 1.5
- norm_bias: float32 [1792], replicated, may hold values from -3 to 3
- w_in: bfloat16 [1792, 15360], P('dp', 'mp'), may hold values from -0.125 to 0.125
- b_in: float32 [15360], P('mp'), may hold values from -3 to 3
- w_out: bfloat16 [15360, 1792], P('mp', 'dp'), may hold values from -0.046875 to 0.046875
- b_out: float32 [1792], replicated, may hold values from -3 to 3
Outputs:
- result: bfloat16 [1280, 1792], P(('dp', 'mp'))
All inputs are finite; a program needn't handle non-finite values.
Results may differ from a plain program's by a relative error of at most 0.0042.
Values may be sent and summed in bfloat16 or wider, within the bound.
A program may use at most 128 MiB of HBM per device.

v0:
```python
import jax
import jax.numpy as jnp
from jax import lax
from jax.sharding import PartitionSpec as P


def on_device(tokens, norm_gain, norm_bias, w_in, b_in, w_out, b_out):
    values = tokens.astype(jnp.float32)
    center = jnp.mean(values, axis=1, keepdims=True)
    spread = jnp.mean((values - center) ** 2, axis=1, keepdims=True)
    normed = ((values - center) / jnp.sqrt(spread + 1e-06) * norm_gain + norm_bias).astype(
        jnp.bfloat16
    )
    w_in_full = lax.all_gather(w_in, "dp", axis=0, tiled=True)
    gathered = lax.all_gather(normed, "mp", axis=0, tiled=True)
    pre = jnp.dot(gathered, w_in_full, preferred_element_type=jnp.float32) + b_in
    hidden = jax.nn.gelu(pre, approximate=False).astype(jnp.bfloat16)
    w_out_full = lax.all_gather(w_out, "dp", axis=1, tiled=True)
    summed = lax.psum_scatter(
        jnp.dot(hidden, w_out_full, preferred_element_type=jnp.float32),
        "mp",
        scatter_dimension=0,
        tiled=True,
    )
    return (values + summed + b_out).astype(jnp.bfloat16)


def solution(mesh):
    placed = (P(("dp", "mp"), None), P(), P(), P("dp", "mp"), P("mp"), P("mp", "dp"), P())
    return jax.shard_map(
        on_device, mesh=mesh, in_specs=placed, out_specs=P(("dp", "mp"), None), check_vma=False
    )
```

profile of v0, /device:TPU:0, one launch (start us, length us, event | category | flops | bytes accessed | tf_op | source)
XLA Modules:
  0.0 249.3 jit_solution(16586171305829466705)
XLA Ops:
  6.5 0.0 copy-start.2
  6.5 0.0 all-gather.4.cloned.1.call-start
  6.5 1.0 convert_reduce_fusion
  7.6 1.1 fusion.45
  8.7 1.7 fusion.48
  10.5 0.0 all-gather.4.cloned.1.call-update
  10.5 0.0 all-gather.6.cloned.1.call-start
  10.5 0.7 all-gather.6.cloned.1.call-update
  11.2 0.0 all-gather.8.cloned.1.call-start
  11.3 0.7 all-gather.8.cloned.1.call-update
  12.0 0.0 copy-start
  12.0 0.0 copy-start.1
  12.0 0.0 reduce-scatter.2.cloned.1.call-start
  12.0 42.5 %all-gather.4.cloned.1.call-done = bf16[320,1792]{1,0:T(8,128)(2,1)} async-done(((bf16[40,1792]{1,0:T(8,128)(2,1)}), bf16[320,1792]{1,0:T(8,128)(2,1)}) %all-gather.4.cloned.1.call-update) | async-done | bytes 1146896 | tf_op jit(solution)/shard_map/all_gather | solution.py:15
  54.6 49.7 %all-gather.6.cloned.1.call-done = bf16[1792,1920]{1,0:T(8,128)(2,1)} async-done(((bf16[448,1920]{1,0:T(8,128)(2,1)}), bf16[1792,1920]{1,0:T(8,128)(2,1)}) %all-gather.6.cloned.1.call-update) | async-done | bytes 6881296 | tf_op jit(solution)/shard_map/all_gather | solution.py:14
  104.3 51.3 %all-gather.8.cloned.1.call-done = bf16[1920,1792]{0,1:T(8,128)(2,1)} async-done(((bf16[1920,448]{0,1:T(8,128)(2,1)}), bf16[1920,1792]{0,1:T(8,128)(2,1)}) %all-gather.8.cloned.1.call-update) | async-done | bytes 6881296 | tf_op jit(solution)/shard_map/all_gather | solution.py:18
  155.6 0.0 copy-done.2
  155.6 15.7 %fusion.10 = f32[320,1792]{1,0:T(8,128)} fusion(bf16[1920,1792]{0,1:T(8,128)(2,1)} %all-gather.8.cloned.1.call-done, bf16[320,1792]{1,0:T(8,128)(2,1)} %all-gather.4.cloned.1.call-done, bf16[1792,1920]{1,0:T(8,128)(2,1)} %all-gather.6.cloned.1.call-done, f32[1920]{0:T(1024)S(1)} %copy-done.2), kind=kOutput, calls=%fused_computation.20 | convolution fusion | flops 4444569600 | bytes 17210880 | tf_op jit(solution)/shard_map/dot_general | solution.py:20
  171.3 0.0 reduce-scatter.2.cloned.1.call-update
  171.4 69.7 %reduce-scatter.2.cloned.1.call-done = f32[40,1792]{1,0:T(8,128)} async-done(((f32[320,1792]{1,0:T(8,128)}), f32[40,1792]{1,0:T(8,128)}) %reduce-scatter.2.cloned.1.call-update) | async-done | bytes 286736 | tf_op jit(solution)/shard_map/reduce_scatter | solution.py:19
  241.1 0.0 copy-done
  241.1 0.0 copy-done.1
  241.1 1.7 fusion.50
  (2 shorter events, 0.0 us)
Async XLA Ops:
  6.5 149.1 %copy-start.2 = (f32[1920]{0:T(1024)S(1)}, f32[1920]{0:T(1024)}, u32[]{:S(2)}) copy-start(f32[1920]{0:T(1024)} %param.11) | copy-start | bytes 23044
  6.5 48.0 %all-gather.4.cloned.1.call-start = ((), (), s32[]{:S(2)}) async-start(), calls=%async_computation.1 | async-start | bytes 1290240 | tf_op jit(solution)/shard_map/all_gather | solution.py:15
  10.5 93.8 %all-gather.6.cloned.1.call-start = ((), (), s32[]{:S(2)}) async-start(), calls=%async_computation.2 | async-start | bytes 8601600 | tf_op jit(solution)/shard_map/all_gather | solution.py:14
  11.2 144.4 %all-gather.8.cloned.1.call-start = ((), (), s32[]{:S(2)}) async-start(), calls=%async_computation.3 | async-start | bytes 8601600 | tf_op jit(solution)/shard_map/all_gather | solution.py:18
  12.0 229.1 %copy-start = (bf16[40,1792]{1,0:T(8,128)(2,1)S(1)}, bf16[40,1792]{1,0:T(8,128)(2,1)}, u32[]{:S(2)}) copy-start(bf16[40,1792]{1,0:T(8,128)(2,1)} %param.7) | copy-start | bytes 430084
  12.0 229.1 %copy-start.1 = (f32[1792]{0:T(1024)S(1)}, f32[1792]{0:T(1024)}, u32[]{:S(2)}) copy-start(f32[1792]{0:T(1024)} %param.13) | copy-start | bytes 21508
  12.0 229.1 %reduce-scatter.2.cloned.1.call-start = ((), (), s32[]{:S(2)}) async-start(), calls=%async_computation.4 | async-start | bytes 2580480 | tf_op jit(solution)/shard_map/reduce_scatter | solution.py:19
Sparse Core Ops, SparseCore 0:
  10.6 43.9 all-gather.3
  56.1 48.1 all-gather.5
  105.9 49.6 all-gather.7
  171.5 69.5 reduce-scatter.1
where the time goes:
time: 249 us
  waiting for transfers between devices  215 us (86%)
  matrix products  15.7 us (6%)
  between operations  13.2 us (5%)
  other arithmetic  5.56 us (2%)
    reduce_scatter x1, waiting for transfers between devices, on_device(): lax.psum_scatter(jnp.dot(hidden, w_out_full, preferred_element_type=jnp.f...  69.7 us
    all_gather x1, waiting for transfers between devices, on_device(): w_out_full = lax.all_gather(w_out, 'dp', axis=1, tiled=True)  51.3 us
    all_gather x1, waiting for transfers between devices, on_device(): w_in_full = lax.all_gather(w_in, 'dp', axis=0, tiled=True)  49.7 us
    all_gather x1, waiting for transfers between devices, on_device(): gathered = lax.all_gather(normed, 'mp', axis=0, tiled=True)  42.5 us
    dot_general x1, matrix products, on_device(): jnp.dot(hidden, w_out_full, preferred_element_type=jnp.float32)  15.7 us
  transfers between devices with their start and end apart: 4, of which 4 were waited for; matrix products, arithmetic and copies ran while one was open for 0% of the time, Pallas kernels for 0%

commit v1 on v0

--- a/solution.py
+++ b/solution.py
@@ -15,7 +15,7 @@
     gathered = lax.all_gather(normed, "mp", axis=0, tiled=True)
     pre = jnp.dot(gathered, w_in_full, preferred_element_type=jnp.float32) + b_in
     hidden = jax.nn.gelu(pre, approximate=False).astype(jnp.bfloat16)
-    w_out_full = lax.all_gather(w_out, "dp", axis=1, tiled=True)
+    w_out_full = jnp.concatenate(lax.all_gather(w_out, "dp"), axis=1)
     summed = lax.psum_scatter(
         jnp.dot(hidden, w_out_full, preferred_element_type=jnp.float32),
         "mp",

time: 249 us -> 249 us (level)
  waiting for transfers between devices: 215 us -> 195 us
  local copies, waits for them, and re-layouts: 0.02 us -> 18.9 us
    all_gather x1, waiting for transfers between devices: 42.5 us -> 24.5 us  [on_device(): gathered = lax.all_gather(normed, 'mp', axis=0, tiled=True)]
    all_gather x0 -> x1, local copies, waits for them, and re-layouts: none -> 12.2 us  [on_device(): w_out_full = jnp.concatenate(lax.all_gather(w_out, 'dp'), axis=1)]
    reshape x0 -> x1, local copies, waits for them, and re-layouts: none -> 6.71 us  [on_device(): w_out_full = jnp.concatenate(lax.all_gather(w_out, 'dp'), axis=1)]
  transfers between devices with their start and end apart: 4 -> 4, of which waited for: 4 -> 4; matrix products, arithmetic and copies ran while one was open for 0% -> 9% of each run, Pallas kernels for 0% -> 0%
where the time goes in v1:
time: 249 us
  waiting for transfers between devices  195 us (78%)
  local copies, waits for them, and re-layouts  18.9 us (8%)
  matrix products  15.8 us (6%)
  between operations  13.1 us (5%)
  other arithmetic  5.55 us (2%)
    reduce_scatter x1, waiting for transfers between devices, on_device(): lax.psum_scatter(jnp.dot(hidden, w_out_full, preferred_element_type=jnp.f...  70 us
    all_gather x1, waiting for transfers between devices, on_device(): w_in_full = lax.all_gather(w_in, 'dp', axis=0, tiled=True)  49.7 us
    all_gather x1, waiting for transfers between devices, on_device(): w_out_full = jnp.concatenate(lax.all_gather(w_out, 'dp'), axis=1)  49.3 us
    all_gather x1, waiting for transfers between devices, on_device(): gathered = lax.all_gather(normed, 'mp', axis=0, tiled=True)  24.5 us
    dot_general x1, matrix products, on_device(): jnp.dot(hidden, w_out_full, preferred_element_type=jnp.float32)  15.8 us
    all_gather x1, local copies, waits for them, and re-layouts, on_device(): w_out_full = jnp.concatenate(lax.all_gather(w_out, 'dp'), axis=1)  12.2 us
    reshape x1, local copies, waits for them, and re-layouts, on_device(): w_out_full = jnp.concatenate(lax.all_gather(w_out, 'dp'), axis=1)  6.71 us
  transfers between devices with their start and end apart: 4, of which 4 were waited for; matrix products, arithmetic and copies ran while one was open for 9% of the time, Pallas kernels for 0%

profile of v1, /device:TPU:0, one launch (start us, length us, event | category | flops | bytes accessed | tf_op | source)
XLA Modules:
  0.0 248.5 jit_solution(16990426359975341822)
XLA Ops:
  6.5 0.0 all-gather.9.cloned.1.call-start
  6.5 0.7 all-gather.9.cloned.1.call-update
  7.3 0.0 all-gather.5.cloned.1.call-start
  7.3 1.0 convert_reduce_fusion
  8.3 1.1 fusion.45
  9.5 1.7 fusion.48
  11.2 0.0 all-gather.5.cloned.1.call-update
  11.2 0.0 all-gather.7.cloned.1.call-start
  11.3 0.7 all-gather.7.cloned.1.call-update
  12.0 0.0 reduce-scatter.2.cloned.1.call-start
  12.0 49.3 %all-gather.9.cloned.1.call-done = bf16[7680,448]{0,1:T(8,128)(2,1)} async-done(((bf16[1920,448]{0,1:T(8,128)(2,1)}), bf16[7680,448]{0,1:T(8,128)(2,1)}) %all-gather.9.cloned.1.call-update) | async-done | bytes 6881296 | tf_op jit(solution)/shard_map/all_gather | solution.py:18
  61.3 12.2 %reshape.24 = bf16[4,1920,448]{1,0,2:T(4,128)(2,1)} reshape(bf16[7680,448]{0,1:T(8,128)(2,1)} %all-gather.9.cloned.1.call-done) | data formatting | bytes 13762560 | tf_op jit(solution)/shard_map/all_gather | solution.py:18
  73.5 0.0 copy-start.2
  73.5 6.7 %copy.8 = bf16[1920,4,448]{0,2,1:T(8,128)(2,1)} copy(bf16[1920,4,448]{0,1,2:T(4,128)(2,1)} %bitcast.7) | data formatting | bytes 13762560 | tf_op jit(solution)/shard_map/reshape | solution.py:18
  80.2 24.5 %all-gather.5.cloned.1.call-done = bf16[320,1792]{1,0:T(8,128)(2,1)} async-done(((bf16[40,1792]{1,0:T(8,128)(2,1)}), bf16[320,1792]{1,0:T(8,128)(2,1)}) %all-gather.5.cloned.1.call-update) | async-done | bytes 1146896 | tf_op jit(solution)/shard_map/all_gather | solution.py:15
  104.7 49.7 %all-gather.7.cloned.1.call-done = bf16[1792,1920]{1,0:T(8,128)(2,1)} async-done(((bf16[448,1920]{1,0:T(8,128)(2,1)}), bf16[1792,1920]{1,0:T(8,128)(2,1)}) %all-gather.7.cloned.1.call-update) | async-done | bytes 6881296 | tf_op jit(solution)/shard_map/all_gather | solution.py:14
  154.5 0.0 copy-done.2
  154.5 0.0 copy-start
  154.5 0.0 copy-start.1
  154.5 15.8 %fusion.10 = f32[320,1792]{1,0:T(8,128)} fusion(bf16[1920,1792]{0,1:T(8,128)(2,1)} %bitcast.8, bf16[320,1792]{1,0:T(8,128)(2,1)} %all-gather.5.cloned.1.call-done, bf16[1792,1920]{1,0:T(8,128)(2,1)} %all-gather.7.cloned.1.call-done, f32[1920]{0:T(1024)S(1)} %copy-done.2), kind=kOutput, calls=%fused_computation.20 | convolution fusion | flops 4444569600 | bytes 17210880 | tf_op jit(solution)/shard_map/dot_general | solution.py:20
  170.3 0.0 reduce-scatter.2.cloned.1.call-update
  170.3 70.0 %reduce-scatter.2.cloned.1.call-done = f32[40,1792]{1,0:T(8,128)} async-done(((f32[320,1792]{1,0:T(8,128)}), f32[40,1792]{1,0:T(8,128)}) %reduce-scatter.2.cloned.1.call-update) | async-done | bytes 286736 | tf_op jit(solution)/shard_map/reduce_scatter | solution.py:19
  240.3 0.0 copy-done
  240.3 0.0 copy-done.1
  240.3 1.7 fusion.50
  (2 shorter events, 0.0 us)
Async XLA Ops:
  6.5 54.8 %all-gather.9.cloned.1.call-start = ((), (), s32[]{:S(2)}) async-start(), calls=%async_computation.4 | async-start | bytes 8601600 | tf_op jit(solution)/shard_map/all_gather | solution.py:18
  7.3 97.5 %all-gather.5.cloned.1.call-start = ((), (), s32[]{:S(2)}) async-start(), calls=%async_computation.1 | async-start | bytes 1290240 | tf_op jit(solution)/shard_map/all_gather | solution.py:15
  11.2 143.3 %all-gather.7.cloned.1.call-start = ((), (), s32[]{:S(2)}) async-start(), calls=%async_computation.2 | async-start | bytes 8601600 | tf_op jit(solution)/shard_map/all_gather | solution.py:14
  12.0 228.4 %reduce-scatter.2.cloned.1.call-start = ((), (), s32[]{:S(2)}) async-start(), calls=%async_computation.3 | async-start | bytes 2580480 | tf_op jit(solution)/shard_map/reduce_scatter | solution.py:19
  73.5 81.0 %copy-start.2 = (f32[1920]{0:T(1024)S(1)}, f32[1920]{0:T(1024)}, u32[]{:S(2)}) copy-start(f32[1920]{0:T(1024)} %param.11) | copy-start | bytes 23044
  154.5 85.8 %copy-start = (bf16[40,1792]{1,0:T(8,128)(2,1)S(1)}, bf16[40,1792]{1,0:T(8,128)(2,1)}, u32[]{:S(2)}) copy-start(bf16[40,1792]{1,0:T(8,128)(2,1)} %param.7) | copy-start | bytes 430084
  154.5 85.8 %copy-start.1 = (f32[1792]{0:T(1024)S(1)}, f32[1792]{0:T(1024)}, u32[]{:S(2)}) copy-start(f32[1792]{0:T(1024)} %param.13) | copy-start | bytes 21508
Sparse Core Ops, SparseCore 0:
  8.9 52.3 all-gather.8
  63.5 41.1 all-gather.4
  106.3 48.1 all-gather.6
  170.4 69.8 reduce-scatter.1
